TPU v7x, 8 devices: a whole 2x2x1 slice. The times are simulated.
8 devices in a mesh: dp: 2 (over y, z), tp: 4 (over x, core).
Axes of the slice: x: 2, y: 2, z: 1, core: 2. Of those that a mesh axis runs over, the one named last changes fastest.
Arguments:
- x: bfloat16 [4096, 5120], P('dp'), parts along dimension 0
- w_gate: bfloat16 [5120, 16384], P(None, 'tp')
- w_up: bfloat16 [5120, 16384], P(None, 'tp')
- w_down: bfloat16 [16384, 5120], P('tp')
Outputs:
- output: bfloat16 [4096, 5120], P('dp'), parts along dimension 0
There are 2 independent parts. A program takes and returns all parts, laid end to end along the dimension named above; an argument that names none is the same for every part.
All inputs are finite; a program needn't handle non-finite values.
Results may differ from a plain program's by a relative error of at most 0.016.
Values are sent between devices in bfloat16 or wider.
A program may use at most 2 GiB of HBM per device.

v0:
```python
import jax
import jax.numpy as jnp
from jax import lax
from jax.sharding import PartitionSpec as P


def solution(mesh):
    def step(x, w_gate, w_up, w_down):
        gate = jnp.dot(x, w_gate, preferred_element_type=jnp.float32)
        up = jnp.dot(x, w_up, preferred_element_type=jnp.float32)
        hidden = (jax.nn.silu(gate) * up).astype(jnp.bfloat16)
        term = jnp.dot(hidden, w_down, preferred_element_type=jnp.float32).astype(jnp.bfloat16)
        return lax.psum(term, "tp")

    return jax.shard_map(
        step,
        mesh=mesh,
        in_specs=(P("dp", None), P(None, "tp"), P(None, "tp"), P("tp", None)),
        out_specs=P("dp", None),
        check_vma=False,
    )
```

profile of v0, /device:TPU:0, one launch (start us, length us, event | category | flops | bytes accessed | tf_op | source)
XLA Modules:
  0.0 682.3 jit_solution(9188859503320940515)
XLA Ops:
  6.5 0.0 all-reduce.2.cloned.1.call-start
  6.5 96.8 %fusion = f32[2048,4096]{1,0:T(8,128)} fusion(bf16[2048,5120]{1,0:T(8,128)(2,1)} %param.4, bf16[5120,4096]{1,0:T(8,128)(2,1)} %param.5), kind=kOutput, calls=%fused_computation.2 | convolution fusion | flops 85899345920 | bytes 96468992 | tf_op jit(solution)/shard_map/dot_general | solution.py:9
  103.3 105.4 %multiply_convert_fusion = bf16[2048,4096]{1,0:T(8,128)(2,1)} fusion(f32[2048,4096]{1,0:T(8,128)} %fusion, bf16[2048,5120]{1,0:T(8,128)(2,1)} %param.4, bf16[5120,4096]{1,0:T(8,128)(2,1)} %param.6), kind=kOutput, calls=%fused_computation | convolution fusion | flops 85949677568 | bytes 113246208 | tf_op jit(solution)/shard_map/dot_general | solution.py:10
  208.7 95.9 %convolution_convert_fusion = bf16[2048,5120]{1,0:T(8,128)(2,1)} fusion(bf16[2048,4096]{1,0:T(8,128)(2,1)} %multiply_convert_fusion, bf16[4096,5120]{1,0:T(8,128)(2,1)} %param.7), kind=kOutput, calls=%fused_computation.1 | convolution fusion | flops 85909831680 | bytes 79691776 | tf_op jit(solution)/shard_map/dot_general | solution.py:12
  304.5 0.0 all-reduce.2.cloned.1.call-update
  304.6 353.6 %all-reduce.2.cloned.1.call-done = bf16[2048,5120]{1,0:T(8,128)(2,1)} async-done(((bf16[2048,5120]{1,0:T(8,128)(2,1)}), bf16[2048,5120]{1,0:T(8,128)(2,1)}) %all-reduce.2.cloned.1.call-update) | async-done | bytes 20971536 | tf_op jit(solution)/shard_map/psum | solution.py:13
  658.1 17.3 %copy.6 = bf16[2048,5120]{1,0:T(8,128)(2,1)} copy(bf16[2048,5120]{1,0:T(8,128)(2,1)} %all-reduce.2.cloned.1.call-done) | data formatting | bytes 41943040
Async XLA Ops:
  6.5 651.6 %all-reduce.2.cloned.1.call-start = ((), (), s32[]{:S(2)}) async-start(), calls=%async_computation | async-start | bytes 41943040 | tf_op jit(solution)/shard_map/psum | solution.py:13
Sparse Core Ops, SparseCore 0:
  304.7 353.3 all-reduce.1
where the time goes:
time: 682 us
  waiting for transfers between devices  354 us (52%)
  matrix products  298 us (44%)
  local copies, waits for them, and re-layouts  17.3 us (3%)
  between operations  13.4 us (2%)
    psum x1, waiting for transfers between devices, step(): return lax.psum(term, 'tp')  354 us
    dot_general x1, matrix products, step(): up = jnp.dot(x, w_up, preferred_element_type=jnp.float32)  105 us
    dot_general x1, matrix products, step(): gate = jnp.dot(x, w_gate, preferred_element_type=jnp.float32)  96.8 us
    dot_general x1, matrix products, step(): jnp.dot(hidden, w_down, preferred_element_type=jnp.float32)  95.9 us
    unnamed x1, local copies, waits for them, and re-layouts  17.3 us
  transfers between devices with their start and end apart: 1, of which 1 were waited for; matrix products, arithmetic and copies ran while one was open for 0% of the time, Pallas kernels for 0%

commit v1 on v0

v1 whole, which is shorter than its diff:
```python
import functools

import jax
import jax.numpy as jnp
from jax import lax
from jax.experimental import pallas as pl
from jax.experimental.pallas import tpu as pltpu
from jax.sharding import PartitionSpec as P

TG = 512
TD = 1024
SLOTS = 3
BF16, F32 = jnp.bfloat16, jnp.float32


def kernel(chunks, x, wg, wu, wd, y, xb, hid, ring, own, snd, rcv, xs, xr, fin,
           x_sem, ring_sem, d2d_s, d2d_r, ici_s, ici_r, fin_l, fin_s, fin_r):
    n_gu, n_d = wg.shape[1] // TG, wd.shape[1] // TD
    depth, ff = x.shape[1], wg.shape[1]
    per = n_gu + n_d
    n_chunks = sum(c for c, _ in chunks)
    me = lax.axis_index("tp")
    core = lax.rem(me, 2)
    partner = {"tp": me + 1 - 2 * core}
    across = {"tp": lax.rem(me + 2, 4)}

    def gu_copies(slot, j):
        cols = pl.ds(pl.multiple_of(j * TG, TG), TG)
        return (
            pltpu.make_async_copy(wg.at[:, cols], ring.at[slot, :, pl.ds(0, TG)], ring_sem.at[slot, 0]),
            pltpu.make_async_copy(wu.at[:, cols], ring.at[slot, :, pl.ds(TG, TG)], ring_sem.at[slot, 1]),
        )

    def d_copy(slot, j):
        cols = pl.ds(pl.multiple_of(j * TD, TD), TD)
        return pltpu.make_async_copy(wd.at[:, cols], ring.at[slot, pl.ds(0, ff), :], ring_sem.at[slot, 0])

    def x_copy(rows, row0, q):
        quarter = rows // 4
        half = lax.rem(q // 2 + core, 2)
        at = pl.multiple_of(row0 + half * (rows // 2) + lax.rem(q, 2) * quarter, quarter)
        return pltpu.make_async_copy(
            x.at[pl.ds(at, quarter), :],
            xb.at[pl.ds(pl.multiple_of(q * quarter, quarter), quarter), :],
            x_sem.at[q],
        )

    def d2d_copy(h, s):
        return pltpu.make_async_remote_copy(
            snd.at[s, pl.ds(0, h), :], rcv.at[s, pl.ds(0, h), :], d2d_s.at[s], d2d_r.at[s],
            device_id=partner, device_id_type=pl.DeviceIdType.MESH)

    def ici_copy(h, p, t):
        tile = (p, pl.ds(0, h), pl.ds(pl.multiple_of(t * TD, TD), TD))
        return pltpu.make_async_remote_copy(
            xs.at[tile], xr.at[tile], ici_s.at[p, t], ici_r.at[p, t],
            device_id=across, device_id_type=pl.DeviceIdType.MESH)

    def fin_copies(h, row0, f, t, k):
        src = fin.at[f, pl.ds(0, h), :]
        dst = y.at[pl.ds(pl.multiple_of(row0 + core * h, h), h), pl.ds(pl.multiple_of(t * TD, TD), TD)]
        return (
            pltpu.make_async_copy(src, dst, fin_l.at[f]),
            pltpu.make_async_remote_copy(
                src, dst, fin_s.at[f], fin_r.at[k],
                device_id=partner, device_id_type=pl.DeviceIdType.MESH),
        )

    def reduce_tile(i, rows, t):
        h, s, p = rows // 2, lax.rem(i * n_d + t, 2), lax.rem(i, 2)
        d2d_copy(h, s).wait_recv()
        total = own[s, pl.ds(0, h), :] + rcv[s, pl.ds(0, h), :].astype(F32)
        xs[p, pl.ds(0, h), pl.ds(pl.multiple_of(t * TD, TD), TD)] = total.astype(BF16)
        ici_copy(h, p, t).start()

    def finish_tile(i, rows, row0, t, prior=None):
        h, p = rows // 2, lax.rem(i, 2)
        k = i * n_d + t
        f = lax.rem(k, 2)
        copy = ici_copy(h, p, t)
        copy.wait_send()
        copy.wait_recv()

        def release(r):
            local, remote = fin_copies(r // 2, 0, f, t, k)
            local.wait()
            remote.wait_send()

        if prior is None:
            pl.when(k >= 2)(lambda: release(rows))
        else:
            release(prior)
        tile = (p, pl.ds(0, h), pl.ds(pl.multiple_of(t * TD, TD), TD))
        fin[f, pl.ds(0, h), :] = (xs[tile].astype(F32) + xr[tile].astype(F32)).astype(BF16)
        for c in fin_copies(h, row0, f, t, k):
            c.start()

    def slot_of(i, s):
        return lax.rem(i * per + s, SLOTS)

    def chunk(i, rows, row0, before, last, following):
        h = rows // 2
        for q in range(4):
            x_copy(rows, row0, q).wait()
        row_before = row0 - before

        @pl.loop(0, n_gu)
        def _(j):
            slot = slot_of(i, j)
            for c in gu_copies(slot, j):
                c.wait()
            ahead = slot_of(i, j + SLOTS - 1)

            @pl.when(j + SLOTS - 1 < n_gu)
            def _():
                for c in gu_copies(ahead, j + SLOTS - 1):
                    c.start()

            @pl.when(j + SLOTS - 1 >= n_gu)
            def _():
                d_copy(ahead, j + SLOTS - 1 - n_gu).start()

            w = TG // 2
            for k in range(2):
                gate = jnp.dot(xb[pl.ds(0, rows), :], ring[slot, :, pl.ds(k * w, w)], preferred_element_type=F32)
                up = jnp.dot(xb[pl.ds(0, rows), :], ring[slot, :, pl.ds(TG + k * w, w)], preferred_element_type=F32)
                hid[pl.ds(0, rows), pl.ds(pl.multiple_of(j * TG + k * w, w), w)] = (
                    gate * jax.nn.sigmoid(gate) * up).astype(BF16)

            @pl.when((j == 0) & (i > 0))
            def _():
                reduce_tile(i - 1, before, n_d - 1)

            @pl.when((lax.rem(j, 2) == 1) & (i > 0))
            def _():
                finish_tile(i - 1, before, row_before, j // 2, None)

        @pl.loop(0, n_d)
        def _(j):
            slot = slot_of(i, n_gu + j)
            d_copy(slot, j).wait()
            ahead = slot_of(i, n_gu + j + SLOTS - 1)

            @pl.when(j + SLOTS - 1 < n_d)
            def _():
                d_copy(ahead, j + SLOTS - 1).start()

            if not last:
                more = (j + SLOTS - 1 >= n_d) & (i + 1 < n_chunks)

                @pl.when(more)
                def _():
                    for c in gu_copies(ahead, j + SLOTS - 1 - n_d):
                        c.start()

                @pl.when(j < 4)
                def _():
                    following(j).start()

            g = i * n_d + j
            s = lax.rem(g, 2)

            @pl.when(g >= 2)
            def _():
                @pl.when(j >= 2)
                def _():
                    d2d_copy(h, s).wait_send()

                @pl.when(j < 2)
                def _():
                    d2d_copy(before // 2, s).wait_send()

            w = TD // 2
            for k in range(2):
                cols = pl.ds(k * w, w)
                term = jnp.dot(hid[pl.ds(0, rows), :], ring[slot, pl.ds(0, ff), cols], preferred_element_type=F32)
                own[s, pl.ds(0, h), cols] = term[:h]
                snd[s, pl.ds(0, h), cols] = term[h:].astype(BF16)

            @pl.when((j == 1) & (i > 0))
            def _():
                finish_tile(i - 1, before, row_before, n_d - 1, None)

            @pl.when(j > 0)
            def _():
                reduce_tile(i, rows, j - 1)

            d2d_copy(h, s).start()

    plan, row = [], 0
    for count, rows in chunks:
        for _ in range(count):
            plan.append((rows, row))
            row += rows

    for q in range(4):
        x_copy(plan[0][0], 0, q).start()
    for j in range(SLOTS - 1):
        for c in gu_copies(j, j):
            c.start()

    barrier = pltpu.get_barrier_semaphore()
    for peer in (partner, across):
        pl.semaphore_signal(barrier, inc=1, device_id=peer, device_id_type=pl.DeviceIdType.MESH)
    pl.semaphore_wait(barrier, 2)

    @pl.loop(0, n_chunks)
    def _(i):
        rows = plan[0][0]
        row0 = pl.multiple_of(i * rows, rows)

        @pl.when(i + 1 < n_chunks)
        def _():
            pass

        chunk(i, rows, row0, rows, False, lambda q: x_copy(rows, lax.rem(i + 1, n_chunks) * rows, q))

    rows, row0 = plan[-1]
    i = n_chunks - 1
    for q in range(4):
        x_copy(rows, 0, q).wait()
    reduce_tile(i, rows, n_d - 1)
    for t in range(n_d):
        finish_tile(i, rows, row0, t, rows)
    for s in range(2):
        d2d_copy(rows // 2, s).wait_send()
        local, remote = fin_copies(rows // 2, 0, s, 0, 0)
        local.wait()
        remote.wait_send()
    for k in range(n_chunks * n_d):
        fin_copies(plan[k // n_d][0] // 2, 0, 0, 0, k)[1].wait_recv()


def solution(mesh):
    chunks = ((4, 512),)
    biggest = max(r for _, r in chunks)
    n_chunks = sum(c for c, _ in chunks)

    def step(x, w_gate, w_up, w_down):
        (rows, depth), ff, width = x.shape, w_gate.shape[1], w_down.shape[1]
        h, n_d = biggest // 2, width // TD
        dma = pltpu.SemaphoreType.DMA
        return pl.pallas_call(
            functools.partial(kernel, chunks),
            out_shape=jax.ShapeDtypeStruct((rows, width), BF16),
            in_specs=[pl.BlockSpec(memory_space=pl.ANY)] * 4,
            out_specs=pl.BlockSpec(memory_space=pl.ANY),
            scratch_shapes=[
                pltpu.VMEM((biggest, depth), BF16),
                pltpu.VMEM((biggest, ff), BF16),
                pltpu.VMEM((SLOTS, depth, 2 * TG), BF16),
                pltpu.VMEM((2, h, TD), F32),
                pltpu.VMEM((2, h, TD), BF16),
                pltpu.VMEM((2, h, TD), BF16),
                pltpu.VMEM((2, h, width), BF16),
                pltpu.VMEM((2, h, width), BF16),
                pltpu.VMEM((2, h, TD), BF16),
                dma((4,)), dma((SLOTS, 2)), dma((2,)), dma((2,)), dma((2, n_d)), dma((2, n_d)),
                dma((2,)), dma((2,)), dma((n_chunks * n_d,)),
            ],
            compiler_params=pltpu.CompilerParams(
                collective_id=0, has_side_effects=True, vmem_limit_bytes=66_900_000),
            cost_estimate=pl.CostEstimate(
                flops=6 * rows * depth * ff, bytes_accessed=4 * 3 * depth * ff * 2, transcendentals=rows * ff),
        )(x, w_gate, w_up, w_down)

    return jax.shard_map(
        step,
        mesh=mesh,
        in_specs=(P("dp", None), P(None, "tp"), P(None, "tp"), P("tp", None)),
        out_specs=P("dp", None),
        check_vma=False,
    )
```

time: 682 us -> 347 us (0.51)
  waiting for transfers between devices: 354 us -> 0 us
  Pallas kernels: 0 us -> 330 us
  matrix products: 298 us -> 0 us
  between operations: 13.4 us -> 0.01 us
    psum x1 -> x0, waiting for transfers between devices: 354 us -> none  [step(): return lax.psum(term, 'tp')]
    pallas_call x0 -> x1, Pallas kernels: none -> 330 us  [step(): pl.pallas_call(functools.partial(kernel, chunks), out_shape=jax.ShapeDtyp...]
    dot_general x3 -> x0, matrix products: 298 us -> none  [the longest x1 105 us: step(): up = jnp.dot(x, w_up, preferred_element_type=jnp.float32)]
  transfers between devices with their start and end apart: 1 -> 0, of which waited for: 1 -> 0; matrix products, arithmetic and copies ran while one was open for 0% -> 0% of each run, Pallas kernels for 0% -> 0%
where the time goes in v1:
time: 347 us
  Pallas kernels  330 us (95%)
  local copies, waits for them, and re-layouts  17.3 us (5%)
    pallas_call x1, Pallas kernels, step(): pl.pallas_call(functools.partial(kernel, chunks), out_shape=jax.ShapeDtyp...  330 us
    unnamed x1, local copies, waits for them, and re-layouts  17.3 us

profile of v1, /device:TPU:0, one launch (start us, length us, event | category | flops | bytes accessed | tf_op | source)
XLA Modules:
  0.0 347.2 jit_solution(4181919736097079680)
XLA Ops:
  0.0 329.9 %shard_map.46 = bf16[2048,5120]{1,0:T(8,128)(2,1)} custom-call(bf16[2048,5120]{1,0:T(8,128)(2,1)} %x.1, bf16[5120,4096]{1,0:T(8,128)(2,1)} %wg.1, bf16[5120,4096]{1,0:T(8,128)(2,1)} %wu.1, bf16[4096,5120]{1,0:T(8,128)(2,1)} %wd.1), custom_call_target="tpu_custom_call" | custom-call | flops 257698037760 | bytes 503316480 | tf_op jit(solution)/shard_map/pallas_call | solution.py:243
  329.9 17.3 %copy.6 = bf16[2048,5120]{1,0:T(8,128)(2,1)} copy(bf16[2048,5120]{1,0:T(8,128)(2,1)} %shard_map.46) | data formatting | bytes 41943040

commit v2 on v0

v2 whole, which is shorter than its diff:
```python
import functools

import jax
import jax.numpy as jnp
from jax import lax
from jax.experimental import pallas as pl
from jax.experimental.pallas import tpu as pltpu
from jax.sharding import PartitionSpec as P

CHUNKS = (512, 512, 448, 320, 256)
TG = 512
TD = 1024
SLOTS = 3
PIECES = 16
BF16, F32 = jnp.bfloat16, jnp.float32


def kernel(x, wg, wu, wd, y, xb, hid, ring, own, snd, rcv, xs0, xs1, xr0, xr1,
           x_sem, ring_sem, d2d_s, d2d_r, ici_s, ici_r, fin_l, fin_s, fin_r, credit):
    ff = wg.shape[1]
    n_gu, n_d = ff // TG, wd.shape[1] // TD
    per = n_gu + n_d
    last = len(CHUNKS) - 1
    first_row = [sum(CHUNKS[:i]) for i in range(len(CHUNKS))]
    xs, xr = (xs0, xs1), (xr0, xr1)
    me = lax.axis_index("tp")
    core = lax.rem(me, 2)
    partner = {"tp": me + 1 - 2 * core}
    across = {"tp": lax.rem(me + 2, 4)}
    remote = functools.partial(pltpu.make_async_remote_copy, device_id_type=pl.DeviceIdType.MESH)

    def block(j, width):
        return pl.ds(pl.multiple_of(j * width, width), width)

    def slot_of(i, s):
        return lax.rem(i * per + s, SLOTS)

    def g_copy(slot, j):
        return pltpu.make_async_copy(wg.at[:, block(j, TG)], ring.at[slot, :, pl.ds(0, TG)], ring_sem.at[slot, 0])

    def u_copy(slot, j):
        return pltpu.make_async_copy(wu.at[:, block(j, TG)], ring.at[slot, :, pl.ds(TG, TG)], ring_sem.at[slot, 1])

    def d_copy(slot, j):
        return pltpu.make_async_copy(wd.at[:, block(j, TD)], ring.at[slot, pl.ds(0, ff), :], ring_sem.at[slot, 0])

    def x_copy(i, q):
        quarter = CHUNKS[i] // 4
        half = lax.rem(q // 2 + core, 2)
        at = pl.multiple_of(first_row[i] + (half * 2 + lax.rem(q, 2)) * quarter, quarter & -quarter)
        return pltpu.make_async_copy(x.at[pl.ds(at, quarter), :], xb.at[block(q, quarter), :], x_sem.at[q])

    def d2d_copy(i, s):
        h = CHUNKS[i] // 2
        return remote(snd.at[s, pl.ds(0, h), :], rcv.at[s, pl.ds(0, h), :], d2d_s.at[s], d2d_r.at[s], device_id=partner)

    def ici_copy(i, t):
        tile = (pl.ds(0, CHUNKS[i] // 2), block(t, TD))
        return remote(xs[i % 2].at[tile], xr[i % 2].at[tile], ici_s.at[i % 2, t], ici_r.at[i % 2, t], device_id=across)

    def fin_refs(i, t):
        h = CHUNKS[i] // 2
        at = pl.multiple_of(first_row[i] + core * h, h & -h)
        return xs[i % 2].at[pl.ds(0, h), block(t, TD)], y.at[pl.ds(at, h), block(t, TD)]

    def fin_here(i, t):
        src, dst = fin_refs(i, t)
        return pltpu.make_async_copy(src, dst, fin_l.at[i % 2, t])

    def fin_there(i, t):
        src, dst = fin_refs(i, t)
        return remote(src, dst, fin_s.at[i % 2, t], fin_r.at[i * n_d + t], device_id=partner)

    def fin_left(i, t):
        fin_here(i, t).wait()
        fin_there(i, t).wait_send()

    def reduce_tile(i, t):
        h, s = CHUNKS[i] // 2, lax.rem(i * n_d + t, 2)
        d2d_copy(i, s).wait_recv()
        if i >= 2:
            fin_left(i - 2, t)
        total = own[s, pl.ds(0, h), :] + rcv[s, pl.ds(0, h), :].astype(F32)
        xs[i % 2][pl.ds(0, h), block(t, TD)] = total.astype(BF16)
        ici_copy(i, t).start()

    def finish_tile(i, t):
        copy = ici_copy(i, t)
        copy.wait_send()
        copy.wait_recv()
        tile = (pl.ds(0, CHUNKS[i] // 2), block(t, TD))
        total = xs[i % 2][tile].astype(F32) + xr[i % 2][tile].astype(F32)
        xs[i % 2][tile] = total.astype(BF16)
        fin_here(i, t).start()
        fin_there(i, t).start()

    for q in range(4):
        x_copy(0, q).start()
    g_copy(0, 0).start()
    u_copy(0, 0).start()

    barrier = pltpu.get_barrier_semaphore()
    for peer in (partner, across):
        pl.semaphore_signal(barrier, inc=1, device_id=peer, device_id_type=pl.DeviceIdType.MESH)
    pl.semaphore_wait(barrier, 2)

    for i, rows in enumerate(CHUNKS):
        h = rows // 2
        for q in range(4):
            x_copy(i, q).wait()

        @pl.loop(0, n_gu)
        def _(j):
            slot, ahead, nxt = slot_of(i, j), slot_of(i, j + SLOTS - 1), j + SLOTS - 1
            g_copy(slot, j).wait()
            u_copy(slot, j).wait()

            if i == 0:

                @pl.when(j == 0)
                def _():
                    for early in range(1, SLOTS - 1):
                        g_copy(early, early).start()
                        u_copy(early, early).start()

            @pl.when(nxt < n_gu)
            def _():
                g_copy(ahead, nxt).start()
                u_copy(ahead, nxt).start()

            @pl.when(nxt >= n_gu)
            def _():
                d_copy(ahead, nxt - n_gu).start()

            w = TG // 2
            for k in range(2):
                gate = jnp.dot(xb[pl.ds(0, rows), :], ring[slot, :, pl.ds(k * w, w)], preferred_element_type=F32)
                up = jnp.dot(xb[pl.ds(0, rows), :], ring[slot, :, pl.ds(TG + k * w, w)], preferred_element_type=F32)
                act = gate * jax.nn.sigmoid(gate) * up
                hid[pl.ds(0, rows), pl.ds(pl.multiple_of(j * TG + k * w, w), w)] = act.astype(BF16)

            if i > 0:

                @pl.when(j == 0)
                def _():
                    reduce_tile(i - 1, n_d - 1)

            if i > 1:

                @pl.when(j < n_d)
                def _():
                    finish_tile(i - 2, j)

                @pl.when(j == n_d - 1)
                def _():
                    pl.semaphore_signal(credit, inc=1, device_id=across, device_id_type=pl.DeviceIdType.MESH)

        @pl.loop(0, n_d)
        def _(j):
            slot, ahead, nxt = slot_of(i, n_gu + j), slot_of(i, n_gu + j + SLOTS - 1), j + SLOTS - 1
            s = lax.rem(i * n_d + j, 2)
            d_copy(slot, j).wait()

            @pl.when(nxt < n_d)
            def _():
                d_copy(ahead, nxt).start()

            if i < last:

                @pl.when(nxt >= n_d)
                def _():
                    g_copy(ahead, nxt - n_d).start()
                    u_copy(ahead, nxt - n_d).start()

                @pl.when(j < 4)
                def _():
                    x_copy(i + 1, j).start()

            @pl.when(j >= 2)
            def _():
                d2d_copy(i, s).wait_send()

            if i > 0:

                @pl.when(j < 2)
                def _():
                    d2d_copy(i - 1, s).wait_send()

            w = TD // 2
            for k in range(2):
                term = jnp.dot(hid[pl.ds(0, rows), :], ring[slot, pl.ds(0, ff), pl.ds(k * w, w)], preferred_element_type=F32)
                own[s, pl.ds(0, h), pl.ds(k * w, w)] = term[:h]
                snd[s, pl.ds(0, h), pl.ds(k * w, w)] = term[h:].astype(BF16)

            if i > 1:

                @pl.when(j == 1)
                def _():
                    pl.semaphore_wait(credit, 1)

            @pl.when(j > 0)
            def _():
                reduce_tile(i, j - 1)

            d2d_copy(i, s).start()

    reduce_tile(last, n_d - 1)
    for i in (last - 1, last):
        for t in range(n_d):
            finish_tile(i, t)
    for s in range(2):
        d2d_copy(last, s).wait_send()
    for i in (last - 1, last):
        for t in range(n_d):
            fin_left(i, t)
    for i in range(len(CHUNKS)):
        for t in range(n_d):
            fin_there(i, t).wait_recv()


def copy_kernel(src, dst, buf, in_sem, out_sem):
    rows = src.shape[0] // PIECES

    def load(p):
        at = pl.ds(p * rows, rows)
        return pltpu.make_async_copy(src.at[at, :], buf.at[at, :], in_sem.at[p])

    def store(p):
        at = pl.ds(p * rows, rows)
        return pltpu.make_async_copy(buf.at[at, :], dst.at[at, :], out_sem.at[p])

    for p in range(PIECES):
        load(p).start()
    for p in range(PIECES):
        load(p).wait()
        store(p).start()
    for p in range(PIECES):
        store(p).wait()


def solution(mesh):
    def step(x, w_gate, w_up, w_down):
        (rows, depth), ff, width = x.shape, w_gate.shape[1], w_down.shape[1]
        big, n_d, n = max(CHUNKS), width // TD, len(CHUNKS)
        h = big // 2
        even, odd = max(CHUNKS[0::2]) // 2, max(CHUNKS[1::2]) // 2
        dma, vmem = pltpu.SemaphoreType.DMA, pltpu.VMEM
        anywhere = pl.BlockSpec(memory_space=pl.ANY)
        summed = pl.pallas_call(
            kernel,
            out_shape=jax.ShapeDtypeStruct((rows, width), BF16),
            in_specs=[anywhere] * 4,
            out_specs=anywhere,
            scratch_shapes=[
                vmem((big, depth), BF16),
                vmem((big, ff), BF16),
                vmem((SLOTS, depth, 2 * TG), BF16),
                vmem((2, h, TD), F32),
                vmem((2, h, TD), BF16),
                vmem((2, h, TD), BF16),
                vmem((even, width), BF16),
                vmem((odd, width), BF16),
                vmem((even, width), BF16),
                vmem((odd, width), BF16),
                dma((4,)), dma((SLOTS, 2)), dma((2,)), dma((2,)), dma((2, n_d)), dma((2, n_d)),
                dma((2, n_d)), dma((2, n_d)), dma((n * n_d,)),
                pltpu.SemaphoreType.REGULAR,
            ],
            compiler_params=pltpu.CompilerParams(
                collective_id=0, has_side_effects=True, vmem_limit_bytes=66_900_000),
            cost_estimate=pl.CostEstimate(
                flops=6 * rows * depth * ff, bytes_accessed=n * 6 * depth * ff, transcendentals=rows * ff),
        )(x, w_gate, w_up, w_down)
        return pl.pallas_call(
            copy_kernel,
            out_shape=jax.ShapeDtypeStruct((rows, width), BF16),
            in_specs=[anywhere],
            out_specs=anywhere,
            scratch_shapes=[vmem((rows, width), BF16), dma((PIECES,)), dma((PIECES,))],
            compiler_params=pltpu.CompilerParams(vmem_limit_bytes=40_000_000),
            cost_estimate=pl.CostEstimate(flops=0, bytes_accessed=4 * rows * width, transcendentals=0),
        )(summed)

    return jax.shard_map(
        step,
        mesh=mesh,
        in_specs=(P("dp", None), P(None, "tp"), P(None, "tp"), P("tp", None)),
        out_specs=P("dp", None),
        check_vma=False,
    )
```

time: 682 us -> 324 us (0.48)
  waiting for transfers between devices: 354 us -> 0 us
  Pallas kernels: 0 us -> 324 us
  matrix products: 298 us -> 0 us
  local copies, waits for them, and re-layouts: 17.3 us -> 0 us
  between operations: 13.4 us -> 0.19 us
    psum x1 -> x0, waiting for transfers between devices: 354 us -> none  [step(): return lax.psum(term, 'tp')]
    pallas_call x0 -> x2, Pallas kernels: none -> 324 us  [the longest x1 309 us: step(): pl.pallas_call(kernel, out_shape=jax.ShapeDtypeStruct((rows, width), BF16...]
    dot_general x3 -> x0, matrix products: 298 us -> none  [the longest x1 105 us: step(): up = jnp.dot(x, w_up, preferred_element_type=jnp.float32)]
    unnamed x1 -> x0, local copies, waits for them, and re-layouts: 17.3 us -> none
  transfers between devices with their start and end apart: 1 -> 0, of which waited for: 1 -> 0; matrix products, arithmetic and copies ran while one was open for 0% -> 0% of each run, Pallas kernels for 0% -> 0%
where the time goes in v2:
time: 324 us
  Pallas kernels  324 us (100%)
    pallas_call x1, Pallas kernels, step(): pl.pallas_call(kernel, out_shape=jax.ShapeDtypeStruct((rows, width), BF16...  309 us
    pallas_call x1, Pallas kernels, step(): pl.pallas_call(copy_kernel, out_shape=jax.ShapeDtypeStruct((rows, width),...  14.7 us

profile of v2, /device:TPU:0, one launch (start us, length us, event | category | flops | bytes accessed | tf_op | source)
XLA Modules:
  0.0 324.1 jit_solution(3758514424050605513)
XLA Ops:
  0.0 309.2 %shard_map.46.src = bf16[2048,5120]{1,0:T(8,128)(2,1)} custom-call(bf16[2048,5120]{1,0:T(8,128)(2,1)} %x.1, bf16[5120,4096]{1,0:T(8,128)(2,1)} %wg.1, bf16[5120,4096]{1,0:T(8,128)(2,1)} %wu.1, bf16[4096,5120]{1,0:T(8,128)(2,1)} %wd.1), custom_call_target="tpu_custom_call" | custom-call | flops 257698037760 | bytes 629145600 | tf_op jit(solution)/shard_map/pallas_call | solution.py:249
  309.2 14.7 %shard_map.47 = bf16[2048,5120]{1,0:T(8,128)(2,1)} custom-call(bf16[2048,5120]{1,0:T(8,128)(2,1)} %shard_map.46.src), custom_call_target="tpu_custom_call" | custom-call | bytes 41943040 | tf_op jit(solution)/shard_map/pallas_call | solution.py:274

commit v3 on v2

--- a/solution.py
+++ b/solution.py
@@ -12,11 +12,13 @@
 TD = 1024
 SLOTS = 3
 PIECES = 16
+COPY_COST = 20_000_000_000
+REST = 3
 BF16, F32 = jnp.bfloat16, jnp.float32
 
 
-def kernel(x, wg, wu, wd, y, xb, hid, ring, own, snd, rcv, xs0, xs1, xr0, xr1,
-           x_sem, ring_sem, d2d_s, d2d_r, ici_s, ici_r, fin_l, fin_s, fin_r, credit):
+def kernel(x, wg, wu, wd, y, rest, xb, hid, ring, own, snd, rcv, xs0, xs1, xr0, xr1,
+           x_sem, ring_sem, d2d_s, d2d_r, ici_s, ici_r, fin_l, fin_s, fin_r, credit, rest_sem):
     ff = wg.shape[1]
     n_gu, n_d = ff // TG, wd.shape[1] // TD
     per = n_gu + n_d
@@ -75,6 +77,11 @@
         fin_here(i, t).wait()
         fin_there(i, t).wait_send()
 
+    def rest_copy(t):
+        k = t - (n_d - REST)
+        src = xs[last % 2].at[pl.ds(0, CHUNKS[last] // 2), block(t, TD)]
+        return pltpu.make_async_copy(src, rest.at[:, block(k, TD)], rest_sem.at[k])
+
     def reduce_tile(i, t):
         h, s = CHUNKS[i] // 2, lax.rem(i * n_d + t, 2)
         d2d_copy(i, s).wait_recv()
@@ -82,7 +89,13 @@
             fin_left(i - 2, t)
         total = own[s, pl.ds(0, h), :] + rcv[s, pl.ds(0, h), :].astype(F32)
         xs[i % 2][pl.ds(0, h), block(t, TD)] = total.astype(BF16)
-        ici_copy(i, t).start()
+        if i < last:
+            ici_copy(i, t).start()
+        elif isinstance(t, int):
+            rest_copy(t).start()
+        else:
+            pl.when(t < n_d - REST)(lambda: ici_copy(i, t).start())
+            pl.when(t >= n_d - REST)(lambda: rest_copy(t).start())
 
     def finish_tile(i, t):
         copy = ici_copy(i, t)
@@ -205,17 +218,22 @@
             d2d_copy(i, s).start()
 
     reduce_tile(last, n_d - 1)
+    def finished(i):
+        return n_d if i < last else n_d - REST
+
     for i in (last - 1, last):
-        for t in range(n_d):
+        for t in range(finished(i)):
             finish_tile(i, t)
     for s in range(2):
         d2d_copy(last, s).wait_send()
     for i in (last - 1, last):
-        for t in range(n_d):
+        for t in range(finished(i)):
             fin_left(i, t)
     for i in range(len(CHUNKS)):
-        for t in range(n_d):
+        for t in range(finished(i)):
             fin_there(i, t).wait_recv()
+    for t in range(n_d - REST, n_d):
+        rest_copy(t).wait()
 
 
 def copy_kernel(src, dst, buf, in_sem, out_sem):
@@ -236,6 +254,20 @@
         store(p).start()
     for p in range(PIECES):
         store(p).wait()
+
+
+def place_kernel(y_in, here, there, y, sem):
+    del y_in
+    h, width = here.shape
+    core = lax.rem(lax.axis_index("tp"), 2)
+    copies = []
+    for k, (src, half) in enumerate(((here, core), (there, 1 - core))):
+        at = pl.multiple_of(y.shape[0] - 2 * h + half * h, h)
+        copies.append(pltpu.make_async_copy(src, y.at[pl.ds(at, h), pl.ds(y.shape[1] - width, width)], sem.at[k]))
+    for c in copies:
+        c.start()
+    for c in copies:
+        c.wait()
 
 
 def solution(mesh):
@@ -246,11 +278,13 @@
         even, odd = max(CHUNKS[0::2]) // 2, max(CHUNKS[1::2]) // 2
         dma, vmem = pltpu.SemaphoreType.DMA, pltpu.VMEM
         anywhere = pl.BlockSpec(memory_space=pl.ANY)
-        summed = pl.pallas_call(
+        left = jax.ShapeDtypeStruct((CHUNKS[-1] // 2, REST * TD), BF16)
+        whole = jax.ShapeDtypeStruct((rows, width), BF16)
+        summed, rest = pl.pallas_call(
             kernel,
-            out_shape=jax.ShapeDtypeStruct((rows, width), BF16),
+            out_shape=(whole, left),
             in_specs=[anywhere] * 4,
-            out_specs=anywhere,
+            out_specs=(anywhere, anywhere),
             scratch_shapes=[
                 vmem((big, depth), BF16),
                 vmem((big, ff), BF16),
@@ -264,22 +298,35 @@
                 vmem((odd, width), BF16),
                 dma((4,)), dma((SLOTS, 2)), dma((2,)), dma((2,)), dma((2, n_d)), dma((2, n_d)),
                 dma((2, n_d)), dma((2, n_d)), dma((n * n_d,)),
-                pltpu.SemaphoreType.REGULAR,
+                pltpu.SemaphoreType.REGULAR, dma((REST,)),
             ],
             compiler_params=pltpu.CompilerParams(
                 collective_id=0, has_side_effects=True, vmem_limit_bytes=66_900_000),
             cost_estimate=pl.CostEstimate(
                 flops=6 * rows * depth * ff, bytes_accessed=n * 6 * depth * ff, transcendentals=rows * ff),
         )(x, w_gate, w_up, w_down)
-        return pl.pallas_call(
+        arrived = lax.ppermute(rest, "tp", [(i, (i + 2) % 4) for i in range(4)])
+        result = pl.pallas_call(
             copy_kernel,
-            out_shape=jax.ShapeDtypeStruct((rows, width), BF16),
+            out_shape=whole,
             in_specs=[anywhere],
             out_specs=anywhere,
             scratch_shapes=[vmem((rows, width), BF16), dma((PIECES,)), dma((PIECES,))],
             compiler_params=pltpu.CompilerParams(vmem_limit_bytes=40_000_000),
-            cost_estimate=pl.CostEstimate(flops=0, bytes_accessed=4 * rows * width, transcendentals=0),
+            cost_estimate=pl.CostEstimate(flops=COPY_COST, bytes_accessed=4 * rows * width, transcendentals=0),
         )(summed)
+        arrived, result = lax.optimization_barrier((arrived, result))
+        here = (rest.astype(F32) + arrived.astype(F32)).astype(BF16)
+        there = lax.ppermute(here, "tp", [(i, i ^ 1) for i in range(4)])
+        return pl.pallas_call(
+            place_kernel,
+            out_shape=whole,
+            in_specs=[anywhere, pl.BlockSpec(memory_space=vmem), pl.BlockSpec(memory_space=vmem)],
+            out_specs=anywhere,
+            scratch_shapes=[dma((2,))],
+            input_output_aliases={0: 0},
+            compiler_params=pltpu.CompilerParams(vmem_limit_bytes=16_000_000),
+        )(result, here, there)
 
     return jax.shard_map(
         step,

time: 324 us -> 316 us (0.975)
  Pallas kernels: 324 us -> 308 us
  waiting for transfers between devices: 0 us -> 7.17 us
    pallas_call x2 -> x3, Pallas kernels: 324 us -> 308 us  [the longest x1 292 us: step(): pl.pallas_call(kernel, out_shape=(whole, left), in_specs=[anywhere] * 4,...]
    ppermute x0 -> x2, waiting for transfers between devices: none -> 7.17 us  [the longest x1 4.9 us: step(): arrived = lax.ppermute(rest, 'tp', [(i, (i + 2) % 4) for i in range(4)])]
  transfers between devices with their start and end apart: 0 -> 2, of which waited for: 0 -> 2; matrix products, arithmetic and copies ran while one was open for 0% -> 0% of each run, Pallas kernels for 0% -> 5%
where the time goes in v3:
time: 316 us
  Pallas kernels  308 us (97%)
  waiting for transfers between devices  7.17 us (2%)
    pallas_call x1, Pallas kernels, step(): pl.pallas_call(kernel, out_shape=(whole, left), in_specs=[anywhere] * 4,...  292 us
    pallas_call x1, Pallas kernels, step(): pl.pallas_call(copy_kernel, out_shape=whole, in_specs=[anywhere], out_spe...  14.8 us
  transfers between devices with their start and end apart: 2, of which 2 were waited for; matrix products, arithmetic and copies ran while one was open for 0% of the time, Pallas kernels for 5%

profile of v3, /device:TPU:0, one launch (start us, length us, event | category | flops | bytes accessed | tf_op | source)
XLA Modules:
  0.0 315.9 jit_solution(15125782817821544892)
XLA Ops:
  0.0 292.3 %shard_map.46 = (bf16[2048,5120]{1,0:T(8,128)(2,1)}, bf16[128,3072]{1,0:T(8,128)(2,1)}) custom-call(bf16[2048,5120]{1,0:T(8,128)(2,1)} %x.1, bf16[5120,4096]{1,0:T(8,128)(2,1)} %wg.1, bf16[5120,4096]{1,0:T(8,128)(2,1)} %wu.1, bf16[4096,5120]{1,0:T(8,128)(2,1)} %wd.1), custom_call_target="tpu_custom_call" | custom-call | flops 257698037760 | bytes 629145600 | tf_op jit(solution)/shard_map/pallas_call | solution.py:283
  292.3 0.0 collective-permute-start
  292.4 0.0 copy-start
  292.4 14.8 %shard_map.47.y_in = bf16[2048,5120]{1,0:T(8,128)(2,1)} custom-call(bf16[2048,5120]{1,0:T(8,128)(2,1)} %get-tuple-element.10.src), custom_call_target="tpu_custom_call" | custom-call | flops 20000000000 | bytes 41943040 | tf_op jit(solution)/shard_map/pallas_call | solution.py:309
  307.2 4.9 %collective-permute-done = bf16[128,3072]{1,0:T(8,128)(2,1)S(1)} collective-permute-done((bf16[128,3072]{1,0:T(8,128)(2,1)}, bf16[128,3072]{1,0:T(8,128)(2,1)S(1)}, u32[]{:S(2)}, u32[]{:S(2)}) %collective-permute-start) | collective-permute-done | bytes 786464 | tf_op jit(solution)/shard_map/ppermute | solution.py:308
  312.1 0.0 copy-done
  312.1 0.2 add_convert_fusion.here
  312.3 0.0 collective-permute-start.1
  312.3 2.3 collective-permute-done.1.there
  314.6 1.2 shard_map.48
Async XLA Ops:
  292.3 19.8 %collective-permute-start = (bf16[128,3072]{1,0:T(8,128)(2,1)}, bf16[128,3072]{1,0:T(8,128)(2,1)S(1)}, u32[]{:S(2)}, u32[]{:S(2)}) collective-permute-start(bf16[128,3072]{1,0:T(8,128)(2,1)} %get-tuple-element.9), channel_id=1, source_target_pairs={{0,2},{1,3},{2,0},{3,1},{4,6},{5,7},{6,4},{7,5}} | collective-permute-start | bytes 2359304 | tf_op jit(solution)/shard_map/ppermute | solution.py:308
  292.4 19.7 %copy-start = (bf16[128,3072]{1,0:T(8,128)(2,1)S(1)}, bf16[128,3072]{1,0:T(8,128)(2,1)}, u32[]{:S(2)}) copy-start(bf16[128,3072]{1,0:T(8,128)(2,1)} %get-tuple-element.9) | copy-start | bytes 2359300
  312.3 2.3 collective-permute-start.1

commit v4 on v3

--- a/solution.py
+++ b/solution.py
@@ -18,7 +18,7 @@
 
 
 def kernel(x, wg, wu, wd, y, rest, xb, hid, ring, own, snd, rcv, xs0, xs1, xr0, xr1,
-           x_sem, ring_sem, d2d_s, d2d_r, ici_s, ici_r, fin_l, fin_s, fin_r, credit, rest_sem):
+           x_sem, ring_sem, d2d_s, d2d_r, ici_s, ici_r, fin_l, fin_s, fin_r, credit, rest_sem, half_sem):
     ff = wg.shape[1]
     n_gu, n_d = ff // TG, wd.shape[1] // TD
     per = n_gu + n_d
@@ -39,6 +39,11 @@
 
     def g_copy(slot, j):
         return pltpu.make_async_copy(wg.at[:, block(j, TG)], ring.at[slot, :, pl.ds(0, TG)], ring_sem.at[slot, 0])
+
+    def half_copy(w, at, k):
+        cols = pl.ds(k * (TG // 2), TG // 2)
+        return pltpu.make_async_copy(
+            w.at[:, cols], ring.at[0, :, pl.ds(at * TG + k * (TG // 2), TG // 2)], half_sem.at[at, k])
 
     def u_copy(slot, j):
         return pltpu.make_async_copy(wu.at[:, block(j, TG)], ring.at[slot, :, pl.ds(TG, TG)], ring_sem.at[slot, 1])
@@ -109,8 +114,8 @@
 
     for q in range(4):
         x_copy(0, q).start()
-    g_copy(0, 0).start()
-    u_copy(0, 0).start()
+    half_copy(wg, 0, 0).start()
+    half_copy(wu, 1, 0).start()
 
     barrier = pltpu.get_barrier_semaphore()
     for peer in (partner, across):
@@ -122,20 +127,33 @@
         for q in range(4):
             x_copy(i, q).wait()
 
-        @pl.loop(0, n_gu)
+        def gate_up(slot, j, k):
+            w = TG // 2
+            gate = jnp.dot(xb[pl.ds(0, rows), :], ring[slot, :, pl.ds(k * w, w)], preferred_element_type=F32)
+            up = jnp.dot(xb[pl.ds(0, rows), :], ring[slot, :, pl.ds(TG + k * w, w)], preferred_element_type=F32)
+            act = gate * jax.nn.sigmoid(gate) * up
+            hid[pl.ds(0, rows), pl.ds(pl.multiple_of(j * TG + k * w, w), w)] = act.astype(BF16)
+
+        if i == 0:
+            half_copy(wg, 0, 0).wait()
+            half_copy(wu, 1, 0).wait()
+            half_copy(wg, 0, 1).start()
+            half_copy(wu, 1, 1).start()
+            g_copy(1, 1).start()
+            gate_up(0, 0, 0)
+            half_copy(wg, 0, 1).wait()
+            half_copy(wu, 1, 1).wait()
+            u_copy(1, 1).start()
+            g_copy(2, 2).start()
+            u_copy(2, 2).start()
+            gate_up(0, 0, 1)
+
+        @pl.loop(1 if i == 0 else 0, n_gu)
         def _(j):
             slot, ahead, nxt = slot_of(i, j), slot_of(i, j + SLOTS - 1), j + SLOTS - 1
             g_copy(slot, j).wait()
             u_copy(slot, j).wait()
 
-            if i == 0:
-
-                @pl.when(j == 0)
-                def _():
-                    for early in range(1, SLOTS - 1):
-                        g_copy(early, early).start()
-                        u_copy(early, early).start()
-
             @pl.when(nxt < n_gu)
             def _():
                 g_copy(ahead, nxt).start()
@@ -145,12 +163,8 @@
             def _():
                 d_copy(ahead, nxt - n_gu).start()
 
-            w = TG // 2
             for k in range(2):
-                gate = jnp.dot(xb[pl.ds(0, rows), :], ring[slot, :, pl.ds(k * w, w)], preferred_element_type=F32)
-                up = jnp.dot(xb[pl.ds(0, rows), :], ring[slot, :, pl.ds(TG + k * w, w)], preferred_element_type=F32)
-                act = gate * jax.nn.sigmoid(gate) * up
-                hid[pl.ds(0, rows), pl.ds(pl.multiple_of(j * TG + k * w, w), w)] = act.astype(BF16)
+                gate_up(slot, j, k)
 
             if i > 0:
 
@@ -205,17 +219,24 @@
                 own[s, pl.ds(0, h), pl.ds(k * w, w)] = term[:h]
                 snd[s, pl.ds(0, h), pl.ds(k * w, w)] = term[h:].astype(BF16)
 
-            if i > 1:
+            if 1 < i < last:
 
                 @pl.when(j == 1)
                 def _():
                     pl.semaphore_wait(credit, 1)
 
-            @pl.when(j > 0)
+            @pl.when(j > (1 if i == last else 0))
             def _():
                 reduce_tile(i, j - 1)
 
             d2d_copy(i, s).start()
+
+            if i == last:
+
+                @pl.when(j == 0)
+                def _():
+                    pl.semaphore_wait(credit, 1)
+                    reduce_tile(i, j)
 
     reduce_tile(last, n_d - 1)
     def finished(i):
@@ -298,7 +319,7 @@
                 vmem((odd, width), BF16),
                 dma((4,)), dma((SLOTS, 2)), dma((2,)), dma((2,)), dma((2, n_d)), dma((2, n_d)),
                 dma((2, n_d)), dma((2, n_d)), dma((n * n_d,)),
-                pltpu.SemaphoreType.REGULAR, dma((REST,)),
+                pltpu.SemaphoreType.REGULAR, dma((REST,)), dma((2, 2)),
             ],
             compiler_params=pltpu.CompilerParams(
                 collective_id=0, has_side_effects=True, vmem_limit_bytes=66_900_000),

time: 316 us -> 314 us (level)
  no operation moved by 1% of the time
where the time goes in v4:
time: 314 us
  Pallas kernels  307 us (98%)
  waiting for transfers between devices  5.87 us (2%)
    pallas_call x1, Pallas kernels, step(): pl.pallas_call(kernel, out_shape=(whole, left), in_specs=[anywhere] * 4,...  291 us
    pallas_call x1, Pallas kernels, step(): pl.pallas_call(copy_kernel, out_shape=whole, in_specs=[anywhere], out_spe...  14.8 us
  transfers between devices with their start and end apart: 2, of which 2 were waited for; matrix products, arithmetic and copies ran while one was open for 0% of the time, Pallas kernels for 5%

profile of v4, /device:TPU:0, one launch (start us, length us, event | category | flops | bytes accessed | tf_op | source)
XLA Modules:
  0.0 314.2 jit_solution(10610044622654731372)
XLA Ops:
  0.0 290.6 %shard_map.46 = (bf16[2048,5120]{1,0:T(8,128)(2,1)}, bf16[128,3072]{1,0:T(8,128)(2,1)}) custom-call(bf16[2048,5120]{1,0:T(8,128)(2,1)} %x.1, bf16[5120,4096]{1,0:T(8,128)(2,1)} %wg.1, bf16[5120,4096]{1,0:T(8,128)(2,1)} %wu.1, bf16[4096,5120]{1,0:T(8,128)(2,1)} %wd.1), custom_call_target="tpu_custom_call" | custom-call | flops 257698037760 | bytes 629145600 | tf_op jit(solution)/shard_map/pallas_call | solution.py:304
  290.6 1.3 collective-permute-start
  291.9 0.0 copy-start
  291.9 14.8 %shard_map.47.y_in = bf16[2048,5120]{1,0:T(8,128)(2,1)} custom-call(bf16[2048,5120]{1,0:T(8,128)(2,1)} %get-tuple-element.10.src), custom_call_target="tpu_custom_call" | custom-call | flops 20000000000 | bytes 41943040 | tf_op jit(solution)/shard_map/pallas_call | solution.py:330
  306.7 3.6 %collective-permute-done = bf16[128,3072]{1,0:T(8,128)(2,1)S(1)} collective-permute-done((bf16[128,3072]{1,0:T(8,128)(2,1)}, bf16[128,3072]{1,0:T(8,128)(2,1)S(1)}, u32[]{:S(2)}, u32[]{:S(2)}) %collective-permute-start) | collective-permute-done | bytes 786464 | tf_op jit(solution)/shard_map/ppermute | solution.py:329
  310.3 0.0 copy-done
  310.3 0.2 add_convert_fusion.here
  310.5 0.0 collective-permute-start.1
  310.6 2.3 collective-permute-done.1.there
  312.8 1.2 shard_map.48
Async XLA Ops:
  290.6 19.8 %collective-permute-start = (bf16[128,3072]{1,0:T(8,128)(2,1)}, bf16[128,3072]{1,0:T(8,128)(2,1)S(1)}, u32[]{:S(2)}, u32[]{:S(2)}) collective-permute-start(bf16[128,3072]{1,0:T(8,128)(2,1)} %get-tuple-element.9), channel_id=1, source_target_pairs={{0,2},{1,3},{2,0},{3,1},{4,6},{5,7},{6,4},{7,5}} | collective-permute-start | bytes 2359304 | tf_op jit(solution)/shard_map/ppermute | solution.py:329
  291.9 18.4 %copy-start = (bf16[128,3072]{1,0:T(8,128)(2,1)S(1)}, bf16[128,3072]{1,0:T(8,128)(2,1)}, u32[]{:S(2)}) copy-start(bf16[128,3072]{1,0:T(8,128)(2,1)} %get-tuple-element.9) | copy-start | bytes 2359300
  310.5 2.3 collective-permute-start.1
